TPU v7x, 256 devices: a whole 4x4x8 slice. The times are simulated.
256 devices in a mesh: expert: 128 (over y_lo, z, x, core), dp: 2 (over y_hi).
Axes of the slice: x: 4, y: 4 (y_hi: 2, y_lo: 2; y = y_hi * 2 + y_lo), z: 8, core: 2. Of those that a mesh axis runs over, the one named last changes fastest.
Arguments:
- tokens: bfloat16 [32768, 2560], P(('expert', 'dp')), may hold values from -6 to 6
- routes: int32 [32768, 6], P(('expert', 'dp')), may hold values from 0 to 31, all different within a row; in each aligned block of 128 rows (0 to 127, 128 to 255, ...) at most 32 rows name the same one
- combine_weight: float32 [32768, 6], P(('expert', 'dp')), may hold values from 0.05 to 1
- owner_plan: int32 [32], replicated, may hold values from 0 to 31, as said below
- w_in: bfloat16 [2, 24576, 2560], P(None, 'expert', 'dp'), may hold values from -0.125 to 0.125
- w_out: bfloat16 [24576, 2560], P('expert', 'dp'), may hold values from -0.21875 to 0.21875
- grad_in: bfloat16 [2, 2, 24576, 2560], P('dp', None, 'expert'), may hold values from -6 to 6
- grad_out: bfloat16 [2, 24576, 2560], P('dp', 'expert'), may hold values from -6 to 6
- first_in: bfloat16 [2, 24576, 2560], P(None, 'expert', 'dp'), may hold values from -3 to 3
- second_in: bfloat16 [2, 24576, 2560], P(None, 'expert', 'dp'), may hold values from 0.25 to 4
- first_out: bfloat16 [24576, 2560], P('expert', 'dp'), may hold values from -3 to 3
- second_out: bfloat16 [24576, 2560], P('expert', 'dp'), may hold values from 0.25 to 4
Outputs:
- combined: bfloat16 [32768, 2560], P(('expert', 'dp'))
- first_in_next: bfloat16 [2, 24576, 2560], P(None, 'expert', 'dp')
- second_in_next: bfloat16 [2, 24576, 2560], P(None, 'expert', 'dp')
- first_out_next: bfloat16 [24576, 2560], P('expert', 'dp')
- second_out_next: bfloat16 [24576, 2560], P('expert', 'dp')
Inputs may be any that keep to these rules, and one draw needn't show every extreme that they name: owner_plan is an involution: exactly 4 pairs of experts trade owners, every other expert maps to itself. `routes`: in the rows of one device (128 rows) no expert is named by more than 32 rows, a bound that some expert reaches in some device.
All inputs are finite; a program needn't handle non-finite values.
Results may differ from a plain program's by a relative error of at most 0.014.
Values may be sent and summed in bfloat16 or wider, within the bound.
No kernel may reach another device: no remote copies, remote signals or barrier semaphores. Data moves between devices by JAX's collectives and lax.ppermute only.
A program may use at most 192 MiB of HBM per device.

v0:
```python
import jax
import jax.numpy as jnp
from jax import lax
from jax.experimental import pallas as pl
from jax.experimental.pallas import tpu as pltpu
from jax.sharding import Mesh
from jax.sharding import PartitionSpec as P


BETA_ONE = 0.9
BETA_TWO = 0.95
LEARNING_RATE = 0.005
EPSILON = 1e-08
CORRECT_FIRST = 1.0 / (1.0 - 0.9**10)
CORRECT_SECOND = 1.0 / (1.0 - 0.95**10)

YL, NZ, XP, XQ, CORES, NDP = 2, 8, 2, 2, 2, 2
AXES = ("yl", "z", "xp", "xq", "c", "dp")
TOK, TOP, D, HALF, HDEV, CAP = 128, 6, 2560, 1280, 192, 32
GROUPS, GROUP_ROWS = 8, 24
HID = 4 * HDEV
SIZES = (CAP, CAP, CAP // 2, CAP // 2, CAP // 2, CAP // 2)
SWAPPED = (3, 5)
SWAP = [(0, 1), (1, 0)]
X_FAR = [(0, 3), (3, 0), (1, 2), (2, 1)]
DIAGONAL = [(yl * 4 + a, (1 - yl) * 4 + b) for yl in range(2) for a, b in X_FAR]
OUTER = [(0, 3), (3, 0), (1, 2), (2, 1)]
OUTER_DIAGONAL = [(a * 2 + dp, b * 2 + 1 - dp) for a, b in DIAGONAL for dp in range(2)]

BF16, F32 = jnp.bfloat16, jnp.float32


def to_x(a):
    return lax.ppermute(a, ("xp", "xq"), X_FAR)


def to_y(a):
    return lax.ppermute(a, "yl", SWAP)


def to_diagonal(a):
    return lax.ppermute(a, ("yl", "xp", "xq"), DIAGONAL)


def to_outer_y(a):
    return lax.ppermute(a, ("yl", "dp"), OUTER)


def to_outer_diagonal(a):
    return lax.ppermute(a, ("yl", "xp", "xq", "dp"), OUTER_DIAGONAL)


def exchange(a, axes):
    return lax.all_to_all(a, axes, 0, 0, tiled=True)


def along_z(a, step):
    return lax.ppermute(a, "z", [(i, (i + step) % NZ) for i in range(NZ)])


def adam_kernel(d_ref, w_in, w_out, g_in, g_out, got_in, got_out, f_in, s_in, f_out, s_out, new, moments, *apart):
    for m in range(3):
        w, ga, gb, f, s = (
            (w_in[m], g_in[0, m], got_in[m], f_in[m], s_in[m])
            if m < 2
            else (w_out[...], g_out[0], got_out[...], f_out[...], s_out[...])
        )
        g = ga.astype(F32) + gb.astype(F32)
        first = BETA_ONE * f.astype(F32) + (1.0 - BETA_ONE) * g
        second = BETA_TWO * s.astype(F32) + (1.0 - BETA_TWO) * g * g
        stepped = w.astype(F32) - LEARNING_RATE * (first * CORRECT_FIRST) / (
            jnp.sqrt(second * CORRECT_SECOND) + EPSILON
        )
        new[m] = apart[m][...] = stepped.astype(BF16)
        for i, moment in enumerate((first, second)):
            for h in range(2):
                moments[i, h, 0, m * GROUP_ROWS : (m + 1) * GROUP_ROWS] = moment[
                    :, h * 640 : (h + 1) * 640
                ].astype(BF16)


def adam(d, w_in, w_out, g_in, g_out, got_in, got_out, f_in, s_in, f_out, s_out):
    block = GROUP_ROWS
    three = pl.BlockSpec((2, block, HALF), lambda i, d: (0, i, 0))
    two = pl.BlockSpec((block, HALF), lambda i, d: (i, 0))
    return pl.pallas_call(
        adam_kernel,
        grid_spec=pltpu.PrefetchScalarGridSpec(
            num_scalar_prefetch=1,
            grid=(GROUPS,),
            in_specs=[
                three,
                two,
                pl.BlockSpec((1, 2, block, HALF), lambda i, d: (0, 0, i, d[0])),
                pl.BlockSpec((1, block, HALF), lambda i, d: (0, i, d[0])),
                three,
                two,
                three,
                three,
                two,
                two,
            ],
            out_specs=[
                pl.BlockSpec((3, block, HALF), lambda i, d: (0, i, 0)),
                pl.BlockSpec((2, 2, 1, 3 * block, 640), lambda i, d: (0, 0, i, 0, 0)),
                two,
                two,
                two,
            ],
        ),
        out_shape=[
            jax.ShapeDtypeStruct((3, HDEV, HALF), BF16),
            jax.ShapeDtypeStruct((2, 2, GROUPS, 3 * block, 640), BF16),
        ]
        + [jax.ShapeDtypeStruct((HDEV, HALF), BF16)] * 3,
        name="adam",
    )(d, w_in, w_out, g_in, g_out, got_in, got_out, f_in, s_in, f_out, s_out)


def unpack_kernel(landed, f_in, s_in, f_out, s_out):
    for i, (inward, outward) in enumerate(((f_in, f_out), (s_in, s_out))):
        for m in range(3):
            for h in range(2):
                part = landed[i, h, 0, m * GROUP_ROWS : (m + 1) * GROUP_ROWS]
                if m < 2:
                    inward[m, :, h * 640 : (h + 1) * 640] = part
                else:
                    outward[:, h * 640 : (h + 1) * 640] = part


def unpack(landed):
    block = GROUP_ROWS
    three = pl.BlockSpec((2, block, HALF), lambda i: (0, i, 0))
    two = pl.BlockSpec((block, HALF), lambda i: (i, 0))
    inward = jax.ShapeDtypeStruct((2, HDEV, HALF), BF16)
    outward = jax.ShapeDtypeStruct((HDEV, HALF), BF16)
    return pl.pallas_call(
        unpack_kernel,
        grid=(GROUPS,),
        in_specs=[pl.BlockSpec((2, 2, 1, 3 * block, 640), lambda i: (0, 0, i, 0, 0))],
        out_specs=[three, three, two, two],
        out_shape=[inward, inward, outward, outward],
        name="unpack",
    )(landed)


def select_kernel(count, experts, *refs):
    messages, outs, (high, low) = refs[:count], refs[count : count + 6], refs[count + 6 :]
    lane = lax.broadcasted_iota(jnp.int32, (TOK, 4 * CAP), 1)
    row = lax.broadcasted_iota(jnp.int32, (TOK, TOK), 0)
    column = lax.broadcasted_iota(jnp.int32, (TOK, TOK), 1)
    before = jnp.where(column < row, 1.0, 0.0).astype(BF16)
    block, slot = lane // CAP, (lane % CAP).astype(F32)
    mine = jnp.where(
        block == 0, experts[0], jnp.where(block == 1, experts[1], jnp.where(block == 2, experts[2], experts[3]))
    ).astype(F32)
    for i, message in enumerate(messages):
        listing = message[:, D:].astype(F32)
        named = jnp.zeros((TOK, 4 * CAP), F32)
        weight = jnp.zeros((TOK, 4 * CAP), F32)
        for k in range(TOP):
            hit = listing[:, k : k + 1] == mine
            value = listing[:, 8 + k : 9 + k] + listing[:, 16 + k : 17 + k]
            named = jnp.where(hit, 1.0, named)
            weight = jnp.where(hit, value, weight)
        rank = jnp.dot(before, named.astype(BF16), preferred_element_type=F32)
        chosen = jnp.where(rank == slot, named, 0.0)
        table = chosen * weight
        top = table.astype(BF16)
        high[i] = top
        low[i] = (table - top.astype(F32)).astype(BF16)
        rows = lax.dot_general(
            chosen.astype(BF16), message[:, :D], (((0,), (0,)), ((), ())), preferred_element_type=F32
        ).astype(BF16)
        begin = 0
        for out, size in zip(outs, SIZES):
            out[i * size : (i + 1) * size] = rows[begin : begin + size]
            begin += size


def select_rows(experts, messages):
    count = len(messages)
    here = pl.BlockSpec(memory_space=pltpu.VMEM)
    outs = pl.pallas_call(
        lambda *refs: select_kernel(count, *refs),
        in_specs=[pl.BlockSpec(memory_space=pltpu.SMEM)] + [here] * count,
        out_specs=[here] * 8,
        out_shape=[jax.ShapeDtypeStruct((count * size, D), BF16) for size in SIZES]
        + [jax.ShapeDtypeStruct((count, TOK, 4 * CAP), BF16)] * 2,
    )(experts, *messages)
    return outs[:6], outs[6:]


def combine_kernel(count, high, low, *refs):
    parts, outs = refs[:6], refs[6:]
    for i in range(count):
        rows = jnp.concatenate(
            [part[i * size : (i + 1) * size] for part, size in zip(parts, SIZES)], axis=0
        )
        total = jnp.dot(high[i], rows, preferred_element_type=F32)
        total = total + jnp.dot(low[i], rows, preferred_element_type=F32)
        outs[i][...] = total.astype(BF16)


def combine_rows(tables, parts):
    count = tables[0].shape[0]
    here = pl.BlockSpec(memory_space=pltpu.VMEM)
    return pl.pallas_call(
        lambda *refs: combine_kernel(count, *refs),
        in_specs=[here] * 8,
        out_specs=[here] * count,
        out_shape=[jax.ShapeDtypeStruct((TOK, D), BF16)] * count,
    )(*tables, *parts)


def ffn_kernel(count, *refs):
    new, far_new, core_new, core_far_new = refs[:4]
    others = refs[4:16]
    rows, outs = refs[16:22], refs[22:28]
    weights, held, result, weight_sem, row_sem, out_sem = refs[28:]
    share = 4 * CAP * count
    step = share // 2

    def moved(arrays, buffer, sem, inward):
        copies, begin = [], 0
        for i, (array, size) in enumerate(zip(arrays, SIZES)):
            place = pl.ds(begin, count * size)
            for h in range(2):
                far = array.at[:, pl.ds(h * HALF, HALF)]
                near = buffer.at[place, pl.ds((1 - h if i in SWAPPED else h) * HALF, HALF)]
                copies.append(pltpu.make_async_copy(*((far, near) if inward else (near, far)), sem.at[i, h]))
            begin += count * size
        return copies

    copies = []
    for m in range(3):
        for q, piece in enumerate((new, far_new, core_new, core_far_new)):
            place = pl.ds(q * HDEV, HDEV)
            copies.append(pltpu.make_async_copy(piece.at[m], weights.at[0, m, place], weight_sem.at[q, 0, m]))
            copies.append(
                pltpu.make_async_copy(others[3 * q + m], weights.at[1, m, place], weight_sem.at[q, 1, m])
            )
    copies += moved(rows, held, row_sem, True)
    for copy in copies:
        copy.start()
    for copy in copies:
        copy.wait()
    nt = (((1,), (1,)), ((), ()))

    def one_block(i, carry):
        begin = pl.multiple_of(i * step, step)
        x0, x1 = held[pl.ds(begin, step), :HALF], held[pl.ds(begin, step), HALF:]

        def project(m):
            return lax.dot_general(x0, weights[0, m], nt, preferred_element_type=F32) + lax.dot_general(
                x1, weights[1, m], nt, preferred_element_type=F32
            )

        hidden = (jax.nn.silu(project(0)) * project(1)).astype(BF16)
        for h in range(2):
            result[pl.ds(begin, step), h * HALF : (h + 1) * HALF] = jnp.dot(
                hidden, weights[h, 2], preferred_element_type=F32
            ).astype(BF16)
        return carry

    lax.fori_loop(0, 2, one_block, 0)
    copies = moved(outs, result, out_sem, False)
    for copy in copies:
        copy.start()
    for copy in copies:
        copy.wait()


def ffn(pieces, rows):
    count = rows[0].shape[0] // CAP
    share = 4 * CAP * count
    anywhere = pl.BlockSpec(memory_space=pl.ANY)
    return pl.pallas_call(
        lambda *refs: ffn_kernel(count, *refs),
        in_specs=[anywhere] * 22,
        out_specs=[anywhere] * 6,
        out_shape=[jax.ShapeDtypeStruct((count * size, D), BF16) for size in SIZES],
        scratch_shapes=[
            pltpu.VMEM((2, 3, HID, HALF), BF16),
            pltpu.VMEM((share, D), BF16),
            pltpu.VMEM((share, D), BF16),
            pltpu.SemaphoreType.DMA((4, 2, 3)),
            pltpu.SemaphoreType.DMA((6, 2)),
            pltpu.SemaphoreType.DMA((6, 2)),
        ],
    )(*pieces, *rows)


def halves(a, d, axis):
    left, right = jnp.split(a, 2, axis=axis)
    return jnp.where(d == 0, left, right), jnp.where(d == 0, right, left)


def plus(a, *others):
    total = a.astype(F32)
    for b in others:
        total = total + b.astype(F32)
    return total.astype(BF16)


MOVES = ((4, to_diagonal), (5, to_outer_diagonal), (2, to_y), (3, to_outer_y), (1, to_x))


def layer(tokens, routes, combine_weight, owner_plan, w_in, w_out, grad_in, grad_out, first_in, second_in, first_out, second_out):
    d = lax.axis_index("dp")
    yl, z, xp = lax.axis_index("yl"), lax.axis_index("z"), lax.axis_index("xp")
    experts = jnp.stack(
        [a * 16 + z * 2 + b for a, b in ((yl, xp), (yl, 1 - xp), (1 - yl, xp), (1 - yl, 1 - xp))]
    ).astype(jnp.int32)

    def permute(a, axis):
        return lax.ppermute(a, axis, SWAP)

    def spread_out(rows):
        got = list(rows)
        for i, move in MOVES:
            got[i] = move(rows[i])
        return got

    high = combine_weight.astype(BF16)
    low = (combine_weight - high.astype(F32)).astype(BF16)
    gap = jnp.zeros((TOK, 2), BF16)
    mine = jnp.concatenate(
        [*halves(tokens, d, 1), routes.astype(BF16), gap, high, gap, low, jnp.zeros((TOK, 106), BF16)], axis=1
    )
    up, down = [mine], [mine]
    for _ in range(3):
        up.append(along_z(up[-1], 1))
        down.append(along_z(down[-1], -1))
    across = jnp.concatenate([along_z(up[3][: TOK // 2], 1), along_z(down[3][TOK // 2 :], -1)], axis=0)

    got_in = permute(halves(grad_in[0], d, 2)[1], "dp")
    got_out = permute(halves(grad_out[0], d, 1)[1], "dp")
    new, moments, *apart = adam(
        d.reshape(1), w_in, w_out, grad_in, grad_out, got_in, got_out, first_in, second_in, first_out, second_out
    )

    def by_matrix(arrays, axis):
        return [permute(a, axis) for a in arrays]

    other = by_matrix(apart, "dp")
    far_new = permute(new, "xq")
    core_new = permute(new, "c")
    far_other = by_matrix(other, "xq")
    core_other = by_matrix(other, "c")
    core_far_new = permute(far_new, "c")
    core_far_other = by_matrix(far_other, "c")
    pieces = [new, far_new, core_new, core_far_new, *other, *far_other, *core_other, *core_far_other]

    near_rows, near_tables = select_rows(experts, [mine, up[1], down[1], up[2], down[2]])
    near_got = spread_out(near_rows)
    far_rows, far_tables = select_rows(experts, [up[3], down[3], across])
    far_got = spread_out(far_rows)

    plane, piece = ("yl", "xp"), (3 * GROUP_ROWS, 640)
    spread = exchange(moments.reshape(4, GROUPS, *piece), plane)
    spread = exchange(spread.transpose(1, 0, 2, 3), "z").reshape(NZ * 4, *piece)
    source = owner_plan.reshape(2, NZ, 2).transpose(1, 0, 2).reshape(NZ * 4)
    source = source % 16 // 2 * 4 + source // 16 * 2 + source % 2
    picked = spread.at[source].get(mode="promise_in_bounds").reshape(NZ, 4, *piece)
    landed = exchange(picked, "z").transpose(1, 0, 2, 3)
    landed = exchange(landed, plane)
    next_moments = unpack(landed.reshape(2, 2, GROUPS, *piece))

    far_done = ffn(pieces, far_got)
    far_back = spread_out(far_done)
    near_done = ffn(pieces, near_got)
    near_back = spread_out(near_done)

    below3, above3, opposite = combine_rows(far_tables, far_back)
    here, below1, above1, below2, above2 = combine_rows(near_tables, near_back)
    rest = TOK // 2
    rising = along_z(opposite[:rest], 1)
    falling = along_z(opposite[rest:], -1)
    rising = jnp.concatenate([plus(above3[:rest], rising), above3[rest:]], axis=0)
    falling = jnp.concatenate([below3[:rest], plus(below3[rest:], falling)], axis=0)
    rising = along_z(rising, 1)
    falling = along_z(falling, -1)
    rising = along_z(plus(above2, rising), 1)
    falling = along_z(plus(below2, falling), -1)
    rising = along_z(plus(above1, rising), 1)
    falling = along_z(plus(below1, falling), -1)
    total = plus(here, rising, falling)
    combined = jnp.where(d == 0, total, jnp.concatenate([total[:, HALF:], total[:, :HALF]], axis=1))
    return (combined, *next_moments)


def solution(mesh):
    fine = Mesh(mesh.devices.reshape(YL, NZ, XP, XQ, CORES, NDP), AXES)
    expert = ("yl", "z", "xp", "xq", "c")
    in_specs = (
        P(AXES, None),
        P(AXES, None),
        P(AXES, None),
        P(),
        P(None, expert, "dp"),
        P(expert, "dp"),
        P("dp", None, expert, None),
        P("dp", expert, None),
        P(None, expert, "dp"),
        P(None, expert, "dp"),
        P(expert, "dp"),
        P(expert, "dp"),
    )
    out_specs = (
        P(AXES, None),
        P(None, expert, "dp"),
        P(None, expert, "dp"),
        P(expert, "dp"),
        P(expert, "dp"),
    )
    return jax.shard_map(layer, mesh=fine, in_specs=in_specs, out_specs=out_specs, check_vma=False)
```

profile of v0, /device:TPU:8, one launch (start us, length us, event | category | flops | bytes accessed | tf_op | source)
XLA Modules:
  0.0 517.9 jit_solution(3441378558602202361)
XLA Ops:
  6.1 31.9 %collective-permute-done.5.got_out = bf16[192,1280]{1,0:T(8,128)(2,1)S(1)} collective-permute-done((bf16[192,1280]{1,0:T(8,128)(2,1)S(1)}, bf16[192,1280]{1,0:T(8,128)(2,1)S(1)}, u32[]{:S(2)}, u32[]{:S(2)}) %collective-permute-start.5) | collective-permute-done | bytes 491552 | tf_op jit(solution)/shard_map/ppermute | solution.py:317
  39.1 9.3 %adam.1 = (bf16[3,192,1280]{2,1,0:T(8,128)(2,1)}, bf16[2,2,8,72,640]{4,3,2,1,0:T(8,128)(2,1)}, bf16[192,1280]{1,0:T(8,128)(2,1)}, bf16[192,1280]{1,0:T(8,128)(2,1)}, bf16[192,1280]{1,0:T(8,128)(2,1)}) custom-call(s32[1]{0:T(128)} %bitcast.4.d_ref, bf16[2,192,1280]{2,1,0:T(8,128)(2,1)} %w_in.1, bf16[192,1280]{1,0:T(8,128)(2,1)} %w_out.1, ...), custom_call_target="tpu_custom_call" | custom-call | tf_op jit(solution)/shard_map/adam/pallas_call | solution.py:86
  48.4 5.8 %all-to-all-start = ((bf16[4,8,72,640]{3,2,1,0:T(8,128)(2,1)}), bf16[4,8,72,640]{3,2,1,0:T(8,128)(2,1)S(1)}, u32[]{:S(2)}, u32[]{:S(2)}) async-start(bf16[4,8,72,640]{3,2,1,0:T(8,128)(2,1)} %bitcast.25), calls=%async_computation | async-start | bytes 5898240 | tf_op jit(solution)/shard_map/all_to_all | solution.py:54
  60.2 28.0 %all-to-all-done = bf16[4,8,72,640]{3,2,1,0:T(8,128)(2,1)S(1)} async-done(((bf16[4,8,72,640]{3,2,1,0:T(8,128)(2,1)}), bf16[4,8,72,640]{3,2,1,0:T(8,128)(2,1)S(1)}, u32[]{:S(2)}, u32[]{:S(2)}) %all-to-all-start) | async-done | bytes 2949152 | tf_op jit(solution)/shard_map/all_to_all | solution.py:54
  90.0 8.5 %all-to-all-start.1 = ((bf16[8,4,72,640]{3,2,1,0:T(8,128)(2,1)}), bf16[8,4,72,640]{3,2,1,0:T(8,128)(2,1)S(1)}, u32[]{:S(2)}, u32[]{:S(2)}) async-start(bf16[8,4,72,640]{3,2,1,0:T(8,128)(2,1)} %bitcast.19), calls=%async_computation.1 | async-start | bytes 5898240 | tf_op jit(solution)/shard_map/all_to_all | solution.py:54
  105.9 71.6 %collective-permute-done.1.refs_3_ = bf16[128,2688]{1,0:T(8,128)(2,1)S(1)} collective-permute-done((bf16[128,2688]{1,0:T(8,128)(2,1)}, bf16[128,2688]{1,0:T(8,128)(2,1)S(1)}, u32[]{:S(2)}, u32[]{:S(2)}) %collective-permute-start.1) | collective-permute-done | bytes 688160 | tf_op jit(solution)/shard_map/ppermute | solution.py:58
  182.7 9.2 %collective-permute-done.11.refs_6_ = bf16[192,1280]{1,0:T(8,128)(2,1)S(1)} collective-permute-done((bf16[192,1280]{1,0:T(8,128)(2,1)}, bf16[192,1280]{1,0:T(8,128)(2,1)S(1)}, u32[]{:S(2)}, u32[]{:S(2)}) %collective-permute-start.11) | collective-permute-done | bytes 491552 | tf_op jit(solution)/shard_map/ppermute | solution.py:317
  196.0 9.4 %collective-permute-done.13.refs_8_ = bf16[192,1280]{1,0:T(8,128)(2,1)} collective-permute-done((bf16[192,1280]{1,0:T(8,128)(2,1)S(1)}, bf16[192,1280]{1,0:T(8,128)(2,1)}, u32[]{:S(2)}, u32[]{:S(2)}) %collective-permute-start.13) | collective-permute-done | bytes 491552 | tf_op jit(solution)/shard_map/ppermute | solution.py:317
  207.8 5.5 %collective-permute-done.14.refs_9_ = bf16[192,1280]{1,0:T(8,128)(2,1)S(1)} collective-permute-done((bf16[192,1280]{1,0:T(8,128)(2,1)S(1)}, bf16[192,1280]{1,0:T(8,128)(2,1)S(1)}, u32[]{:S(2)}, u32[]{:S(2)}) %collective-permute-start.14) | collective-permute-done | bytes 491552 | tf_op jit(solution)/shard_map/ppermute | solution.py:317
  230.5 4.4 shard_map.158
  244.9 12.3 %collective-permute-done.38.refs_20_ = bf16[48,2560]{1,0:T(8,128)(2,1)S(1)} collective-permute-done((bf16[48,2560]{1,0:T(8,128)(2,1)}, bf16[48,2560]{1,0:T(8,128)(2,1)S(1)}, u32[]{:S(2)}, u32[]{:S(2)}) %collective-permute-start.38) | collective-permute-done | bytes 245792 | tf_op jit(solution)/shard_map/ppermute | solution.py:42
  261.9 13.5 %shard_map.159 = (bf16[96,2560]{1,0:T(8,128)(2,1)}, bf16[96,2560]{1,0:T(8,128)(2,1)}, bf16[48,2560]{1,0:T(8,128)(2,1)}, bf16[48,2560]{1,0:T(8,128)(2,1)}, bf16[4...) custom-call(bf16[3,192,1280]{2,1,0:T(8,128)(2,1)} %get-tuple-element.52.refs_0_, ...), custom_call_target="tpu_custom_call" | custom-call | tf_op jit(solution)/shard_map/pallas_call | solution.py:278
  283.0 6.1 %shard_map.155 = (bf16[160,2560]{1,0:T(8,128)(2,1)}, bf16[160,2560]{1,0:T(8,128)(2,1)}, bf16[80,2560]{1,0:T(8,128)(2,1)}, bf16[80,2560]{1,0:T(8,128)(2,1)}, bf16...) custom-call(s32[4]{0:T(128)} %pad_add_fusion.refs_0_, ...), custom_call_target="tpu_custom_call" | custom-call | tf_op jit(solution)/shard_map/pallas_call | solution.py:184
  312.4 16.0 %collective-permute-done.24.refs_20_ = bf16[80,2560]{1,0:T(8,128)(2,1)} collective-permute-done((bf16[80,2560]{1,0:T(8,128)(2,1)}, bf16[80,2560]{1,0:T(8,128)(2,1)}, u32[]{:S(2)}, u32[]{:S(2)}) %collective-permute-start.24) | collective-permute-done | bytes 409632 | tf_op jit(solution)/shard_map/ppermute | solution.py:42
  328.5 7.2 %collective-permute-done.25.refs_21_ = bf16[80,2560]{1,0:T(8,128)(2,1)} collective-permute-done((bf16[80,2560]{1,0:T(8,128)(2,1)}, bf16[80,2560]{1,0:T(8,128)(2,1)}, u32[]{:S(2)}, u32[]{:S(2)}) %collective-permute-start.25) | collective-permute-done | bytes 409632 | tf_op jit(solution)/shard_map/ppermute | solution.py:50
  335.6 15.4 %shard_map.156 = (bf16[160,2560]{1,0:T(8,128)(2,1)}, bf16[160,2560]{1,0:T(8,128)(2,1)}, bf16[80,2560]{1,0:T(8,128)(2,1)}, bf16[80,2560]{1,0:T(8,128)(2,1)}, bf16...) custom-call(bf16[3,192,1280]{2,1,0:T(8,128)(2,1)} %get-tuple-element.52.refs_0_, ...), custom_call_target="tpu_custom_call" | custom-call | tf_op jit(solution)/shard_map/pallas_call | solution.py:278
  362.5 5.9 %all-to-all-start.2 = ((bf16[8,4,72,640]{3,2,1,0:T(8,128)(2,1)}), bf16[8,4,72,640]{3,2,1,0:T(8,128)(2,1)S(1)}, u32[]{:S(2)}, u32[]{:S(2)}) async-start(bf16[8,4,72,640]{3,2,1,0:T(8,128)(2,1)} %bitcast.21), calls=%async_computation.2 | async-start | bytes 5898240 | tf_op jit(solution)/shard_map/all_to_all | solution.py:54
  376.8 62.2 %collective-permute-done.49 = bf16[64,2560]{1,0:T(8,128)(2,1)S(1)} collective-permute-done((bf16[64,2560]{1,0:T(8,128)(2,1)}, bf16[64,2560]{1,0:T(8,128)(2,1)S(1)}, u32[]{:S(2)}, u32[]{:S(2)}) %collective-permute-start.49) | collective-permute-done | bytes 327712 | tf_op jit(solution)/shard_map/ppermute | solution.py:58
  443.2 4.7 shard_map.157
  447.9 5.9 %collective-permute-done.46 = bf16[128,2560]{1,0:T(8,128)(2,1)} collective-permute-done((bf16[128,2560]{1,0:T(8,128)(2,1)}, bf16[128,2560]{1,0:T(8,128)(2,1)}, u32[]{:S(2)}, u32[]{:S(2)}) %collective-permute-start.46) | collective-permute-done | bytes 655392 | tf_op jit(solution)/shard_map/ppermute | solution.py:58
  459.9 9.1 %collective-permute-done.47 = bf16[128,2560]{1,0:T(8,128)(2,1)S(1)} collective-permute-done((bf16[128,2560]{1,0:T(8,128)(2,1)S(1)}, bf16[128,2560]{1,0:T(8,128)(2,1)S(1)}, u32[]{:S(2)}, u32[]{:S(2)}) %collective-permute-start.47) | collective-permute-done | bytes 655392 | tf_op jit(solution)/shard_map/ppermute | solution.py:58
  476.4 4.6 all-to-all-start.3
  486.4 23.4 %all-to-all-done.3 = bf16[4,8,72,640]{3,2,1,0:T(8,128)(2,1)S(1)} async-done(((bf16[4,8,72,640]{3,2,1,0:T(8,128)(2,1)}), bf16[4,8,72,640]{3,2,1,0:T(8,128)(2,1)S(1)}, u32[]{:S(2)}, u32[]{:S(2)}) %all-to-all-start.3) | async-done | bytes 2949152 | tf_op jit(solution)/shard_map/all_to_all | solution.py:54
  511.4 6.0 %unpack.1 = (bf16[2,192,1280]{2,1,0:T(8,128)(2,1)}, bf16[2,192,1280]{2,1,0:T(8,128)(2,1)}, bf16[192,1280]{1,0:T(8,128)(2,1)}, bf16[192,1280]{1,0:T(8,128)(2,1)}) custom-call(bf16[2,2,8,72,640]{4,3,2,1,0:T(8,128)(2,1)} %bitcast.22), custom_call_target="tpu_custom_call" | custom-call | tf_op jit(solution)/shard_map/unpack/pallas_call | solution.py:137
  (197 shorter events, 140.6 us)
Async XLA Ops:
  2.3 35.6 %collective-permute-start.4 = (bf16[2,192,1280]{2,1,0:T(8,128)(2,1)S(1)}, bf16[2,192,1280]{2,1,0:T(8,128)(2,1)S(1)}, u32[]{:S(2)}, u32[]{:S(2)}) collective-permute-start(bf16[2,192,1280]{2,1,0:T(8,128)(2,1)S(1)} %slice_select_fusion), channel_id=1, source_target_pairs={{0,1},{1,0},{2,3},{3,2},{4,5},{5,4},{6,7},{7,6},{8,9},{9,8},{10,11... | collective-permute-start | bytes 2949128 | tf_op jit(solution)/shard_map/ppermute | solution.py:317
  4.8 33.2 %collective-permute-start.5 = (bf16[192,1280]{1,0:T(8,128)(2,1)S(1)}, bf16[192,1280]{1,0:T(8,128)(2,1)S(1)}, u32[]{:S(2)}, u32[]{:S(2)}) collective-permute-start(bf16[192,1280]{1,0:T(8,128)(2,1)S(1)} %slice_select_fusion.1), channel_id=1, source_target_pairs={{0,1},{1,0},{2,3},{3,2},{4,5},{5,4},{6,7},{7,6},{8,9},{9,8},{10,11... | collective-permute-start | bytes 1474568 | tf_op jit(solution)/shard_map/ppermute | solution.py:317
  48.4 39.8 %all-to-all-start = ((bf16[4,8,72,640]{3,2,1,0:T(8,128)(2,1)}), bf16[4,8,72,640]{3,2,1,0:T(8,128)(2,1)S(1)}, u32[]{:S(2)}, u32[]{:S(2)}) async-start(bf16[4,8,72,640]{3,2,1,0:T(8,128)(2,1)} %bitcast.25), calls=%async_computation | async-start | bytes 5898240 | tf_op jit(solution)/shard_map/all_to_all | solution.py:54
  58.3 43.4 %collective-permute-start = (bf16[128,2688]{1,0:T(8,128)(2,1)}, bf16[128,2688]{1,0:T(8,128)(2,1)}, u32[]{:S(2)}, u32[]{:S(2)}) collective-permute-start(bf16[128,2688]{1,0:T(8,128)(2,1)} %concatenate.15.refs_1_), channel_id=1, source_target_pairs={{0,16},{16,32},{32,48},{48,64},{64,80},{80,96},{96,112},{112,0},{1... | collective-permute-start | bytes 2064392 | tf_op jit(solution)/shard_map/ppermute | solution.py:58
  90.0 270.0 %all-to-all-start.1 = ((bf16[8,4,72,640]{3,2,1,0:T(8,128)(2,1)}), bf16[8,4,72,640]{3,2,1,0:T(8,128)(2,1)S(1)}, u32[]{:S(2)}, u32[]{:S(2)}) async-start(bf16[8,4,72,640]{3,2,1,0:T(8,128)(2,1)} %bitcast.19), calls=%async_computation.1 | async-start | bytes 5898240 | tf_op jit(solution)/shard_map/all_to_all | solution.py:54
  98.5 79.0 %collective-permute-start.1 = (bf16[128,2688]{1,0:T(8,128)(2,1)}, bf16[128,2688]{1,0:T(8,128)(2,1)S(1)}, u32[]{:S(2)}, u32[]{:S(2)}) collective-permute-start(bf16[128,2688]{1,0:T(8,128)(2,1)} %concatenate.15.refs_1_), channel_id=1, source_target_pairs={{0,112},{16,0},{32,16},{48,32},{64,48},{80,64},{96,80},{112,96},{1... | collective-permute-start | bytes 2064392 | tf_op jit(solution)/shard_map/ppermute | solution.py:58
  101.7 76.6 %collective-permute-start.2 = (bf16[128,2688]{1,0:T(8,128)(2,1)}, bf16[128,2688]{1,0:T(8,128)(2,1)S(1)}, u32[]{:S(2)}, u32[]{:S(2)}) collective-permute-start(bf16[128,2688]{1,0:T(8,128)(2,1)} %collective-permute-done.refs_2_), channel_id=1, source_target_pairs={{0,16},{16,32},{32,48},{48,64},{64,80},{80,96},{96,112},{112,0},{1... | collective-permute-start | bytes 2064392 | tf_op jit(solution)/shard_map/ppermute | solution.py:58
  101.7 78.9 %collective-permute-start.9 = (bf16[192,1280]{1,0:T(8,128)(2,1)}, bf16[192,1280]{1,0:T(8,128)(2,1)S(1)}, u32[]{:S(2)}, u32[]{:S(2)}) collective-permute-start(bf16[192,1280]{1,0:T(8,128)(2,1)} %get-tuple-element.53), channel_id=1, source_target_pairs={{0,1},{1,0},{2,3},{3,2},{4,5},{5,4},{6,7},{7,6},{8,9},{9,8},{10,11... | collective-permute-start | bytes 1474568 | tf_op jit(solution)/shard_map/ppermute | solution.py:317
  104.0 77.2 %collective-permute-start.10 = (bf16[192,1280]{1,0:T(8,128)(2,1)}, bf16[192,1280]{1,0:T(8,128)(2,1)S(1)}, u32[]{:S(2)}, u32[]{:S(2)}) collective-permute-start(bf16[192,1280]{1,0:T(8,128)(2,1)} %get-tuple-element.54), channel_id=1, source_target_pairs={{0,1},{1,0},{2,3},{3,2},{4,5},{5,4},{6,7},{7,6},{8,9},{9,8},{10,11... | collective-permute-start | bytes 1474568 | tf_op jit(solution)/shard_map/ppermute | solution.py:317
  105.3 109.5 %collective-permute-start.6 = (bf16[3,192,1280]{2,1,0:T(8,128)(2,1)}, bf16[3,192,1280]{2,1,0:T(8,128)(2,1)}, u32[]{:S(2)}, u32[]{:S(2)}) collective-permute-start(bf16[3,192,1280]{2,1,0:T(8,128)(2,1)} %get-tuple-element.52.refs_0_), channel_id=1, source_target_pairs={{0,4},{4,0},{1,5},{5,1},{2,6},{6,2},{3,7},{7,3},{8,12},{12,8},{9,1... | collective-permute-start | bytes 4423688 | tf_op jit(solution)/shard_map/ppermute | solution.py:317
  214.8 46.3 %collective-permute-start.8 = (bf16[3,192,1280]{2,1,0:T(8,128)(2,1)}, bf16[3,192,1280]{2,1,0:T(8,128)(2,1)}, u32[]{:S(2)}, u32[]{:S(2)}) collective-permute-start(bf16[3,192,1280]{2,1,0:T(8,128)(2,1)} %collective-permute-done.6.refs_1_), channel_id=1, source_target_pairs={{0,2},{2,0},{1,3},{3,1},{4,6},{6,4},{5,7},{7,5},{8,10},{10,8},{9,1... | collective-permute-start | bytes 4423688 | tf_op jit(solution)/shard_map/ppermute | solution.py:317
  236.1 24.9 %collective-permute-start.35 = (bf16[96,2560]{1,0:T(8,128)(2,1)}, bf16[96,2560]{1,0:T(8,128)(2,1)S(1)}, u32[]{:S(2)}, u32[]{:S(2)}) collective-permute-start(bf16[96,2560]{1,0:T(8,128)(2,1)} %get-tuple-element.74), channel_id=1, source_target_pairs={{0,12},{12,0},{4,8},{8,4},{1,13},{13,1},{5,9},{9,5},{2,14},{14,2},... | collective-permute-start | bytes 1474568 | tf_op jit(solution)/shard_map/ppermute | solution.py:34
  275.4 29.3 %collective-permute-start.40 = (bf16[96,2560]{1,0:T(8,128)(2,1)}, bf16[96,2560]{1,0:T(8,128)(2,1)S(1)}, u32[]{:S(2)}, u32[]{:S(2)}) collective-permute-start(bf16[96,2560]{1,0:T(8,128)(2,1)} %get-tuple-element.80), channel_id=1, source_target_pairs={{0,12},{12,0},{4,8},{8,4},{1,13},{13,1},{5,9},{9,5},{2,14},{14,2},... | collective-permute-start | bytes 1474568 | tf_op jit(solution)/shard_map/ppermute | solution.py:34
  289.1 46.5 %collective-permute-start.21 = (bf16[160,2560]{1,0:T(8,128)(2,1)}, bf16[160,2560]{1,0:T(8,128)(2,1)}, u32[]{:S(2)}, u32[]{:S(2)}) collective-permute-start(bf16[160,2560]{1,0:T(8,128)(2,1)} %get-tuple-element.57), channel_id=1, source_target_pairs={{0,12},{12,0},{4,8},{8,4},{1,13},{13,1},{5,9},{9,5},{2,14},{14,2},... | collective-permute-start | bytes 2457608 | tf_op jit(solution)/shard_map/ppermute | solution.py:34
  302.5 25.9 %collective-permute-start.24 = (bf16[80,2560]{1,0:T(8,128)(2,1)}, bf16[80,2560]{1,0:T(8,128)(2,1)}, u32[]{:S(2)}, u32[]{:S(2)}) collective-permute-start(bf16[80,2560]{1,0:T(8,128)(2,1)} %get-tuple-element.60), channel_id=1, source_target_pairs={{0,140},{12,128},{4,136},{8,132},{128,12},{140,0},{132,8},{136,4},... | collective-permute-start | bytes 1228808 | tf_op jit(solution)/shard_map/ppermute | solution.py:42
  304.8 30.9 %collective-permute-start.25 = (bf16[80,2560]{1,0:T(8,128)(2,1)}, bf16[80,2560]{1,0:T(8,128)(2,1)}, u32[]{:S(2)}, u32[]{:S(2)}) collective-permute-start(bf16[80,2560]{1,0:T(8,128)(2,1)} %get-tuple-element.61), channel_id=1, source_target_pairs={{0,141},{1,140},{12,129},{13,128},{4,137},{5,136},{8,133},{9,132},... | collective-permute-start | bytes 1228808 | tf_op jit(solution)/shard_map/ppermute | solution.py:50
  312.4 56.1 %collective-permute-start.45 = (bf16[64,2560]{1,0:T(8,128)(2,1)}, bf16[64,2560]{1,0:T(8,128)(2,1)}, u32[]{:S(2)}, u32[]{:S(2)}) collective-permute-start(bf16[64,2560]{1,0:T(8,128)(2,1)} %get-tuple-element.99), channel_id=1, source_target_pairs={{0,16},{16,32},{32,48},{48,64},{64,80},{80,96},{96,112},{112,0},{1... | collective-permute-start | bytes 983048 | tf_op jit(solution)/shard_map/ppermute | solution.py:58
  351.0 92.2 %collective-permute-start.26 = (bf16[160,2560]{1,0:T(8,128)(2,1)}, bf16[160,2560]{1,0:T(8,128)(2,1)}, u32[]{:S(2)}, u32[]{:S(2)}) collective-permute-start(bf16[160,2560]{1,0:T(8,128)(2,1)} %get-tuple-element.63), channel_id=1, source_target_pairs={{0,12},{12,0},{4,8},{8,4},{1,13},{13,1},{5,9},{9,5},{2,14},{14,2},... | collective-permute-start | bytes 2457608 | tf_op jit(solution)/shard_map/ppermute | solution.py:34
  354.4 87.0 %collective-permute-start.28 = (bf16[80,2560]{1,0:T(8,128)(2,1)}, bf16[80,2560]{1,0:T(8,128)(2,1)}, u32[]{:S(2)}, u32[]{:S(2)}) collective-permute-start(bf16[80,2560]{1,0:T(8,128)(2,1)} %get-tuple-element.65), channel_id=1, source_target_pairs={{0,129},{129,0},{1,128},{128,1},{2,131},{131,2},{3,130},{130,3},{4... | collective-permute-start | bytes 1228808 | tf_op jit(solution)/shard_map/ppermute | solution.py:46
  354.4 88.8 %collective-permute-start.29 = (bf16[80,2560]{1,0:T(8,128)(2,1)}, bf16[80,2560]{1,0:T(8,128)(2,1)}, u32[]{:S(2)}, u32[]{:S(2)}) collective-permute-start(bf16[80,2560]{1,0:T(8,128)(2,1)} %get-tuple-element.66), channel_id=1, source_target_pairs={{0,140},{12,128},{4,136},{8,132},{128,12},{140,0},{132,8},{136,4},... | collective-permute-start | bytes 1228808 | tf_op jit(solution)/shard_map/ppermute | solution.py:42
  362.5 112.1 %all-to-all-start.2 = ((bf16[8,4,72,640]{3,2,1,0:T(8,128)(2,1)}), bf16[8,4,72,640]{3,2,1,0:T(8,128)(2,1)S(1)}, u32[]{:S(2)}, u32[]{:S(2)}) async-start(bf16[8,4,72,640]{3,2,1,0:T(8,128)(2,1)} %bitcast.21), calls=%async_computation.2 | async-start | bytes 5898240 | tf_op jit(solution)/shard_map/all_to_all | solution.py:54
  368.5 70.5 %collective-permute-start.49 = (bf16[64,2560]{1,0:T(8,128)(2,1)}, bf16[64,2560]{1,0:T(8,128)(2,1)S(1)}, u32[]{:S(2)}, u32[]{:S(2)}) collective-permute-start(bf16[64,2560]{1,0:T(8,128)(2,1)} %get-tuple-element.100), channel_id=1, source_target_pairs={{0,112},{16,0},{32,16},{48,32},{64,48},{80,64},{96,80},{112,96},{1... | collective-permute-start | bytes 983048 | tf_op jit(solution)/shard_map/ppermute | solution.py:58
  374.8 68.4 %collective-permute-start.30 = (bf16[80,2560]{1,0:T(8,128)(2,1)S(1)}, bf16[80,2560]{1,0:T(8,128)(2,1)}, u32[]{:S(2)}, u32[]{:S(2)}) collective-permute-start(bf16[80,2560]{1,0:T(8,128)(2,1)S(1)} %copy-done.30), channel_id=1, source_target_pairs={{0,141},{1,140},{12,129},{13,128},{4,137},{5,136},{8,133},{9,132},... | collective-permute-start | bytes 1228808 | tf_op jit(solution)/shard_map/ppermute | solution.py:50
  476.4 33.5 %all-to-all-start.3 = ((bf16[4,8,72,640]{3,2,1,0:T(8,128)(2,1)}), bf16[4,8,72,640]{3,2,1,0:T(8,128)(2,1)S(1)}, u32[]{:S(2)}, u32[]{:S(2)}) async-start(bf16[4,8,72,640]{3,2,1,0:T(8,128)(2,1)} %copy.32), calls=%async_computation.3 | async-start | bytes 5898240 | tf_op jit(solution)/shard_map/all_to_all | solution.py:54
  (64 other events, 902.2 us)
where the time goes:
time: 527 us; the launch traced here: 518 us
  waiting for transfers between devices  320 us (61%)
  starting transfers between devices  96.9 us (18%)
  Pallas kernels  62.9 us (12%)
  local copies, waits for them, and re-layouts  19.3 us (4%)
  other arithmetic  17.7 us (3%)
    ppermute x16, waiting for transfers between devices, along_z(): return lax.ppermute(a, 'z', [(i, (i + step) % NZ) for i in range(NZ)])  159 us
    ppermute x17, waiting for transfers between devices, permute(): return lax.ppermute(a, axis, SWAP)  58.3 us
    all_to_all x4, waiting for transfers between devices, exchange(): return lax.all_to_all(a, axes, 0, 0, tiled=True)  51.4 us
    ppermute x4, waiting for transfers between devices, to_diagonal(): return lax.ppermute(a, ('yl', 'xp', 'xq'), DIAGONAL)  32.1 us
    pallas_call x2, Pallas kernels, ffn(): pl.pallas_call(lambda *refs: ffn_kernel(count, *refs), in_specs=[anywhere...  28.9 us
    ppermute x16, starting transfers between devices, along_z(): return lax.ppermute(a, 'z', [(i, (i + step) % NZ) for i in range(NZ)])  26.2 us
    all_to_all x4, starting transfers between devices, exchange(): return lax.all_to_all(a, axes, 0, 0, tiled=True)  24.7 us
    ppermute x4, waiting for transfers between devices, to_outer_diagonal(): return lax.ppermute(a, ('yl', 'xp', 'xq', 'dp'), OUTER_DIAGONAL)  14.9 us
  transfers between devices with their start and end apart: 57, of which 24 were waited for; matrix products, arithmetic and copies ran while one was open for 6% of the time, Pallas kernels for 9%

commit v1 on v0

--- a/solution.py
+++ b/solution.py
@@ -17,6 +17,7 @@
 YL, NZ, XP, XQ, CORES, NDP = 2, 8, 2, 2, 2, 2
 AXES = ("yl", "z", "xp", "xq", "c", "dp")
 TOK, TOP, D, HALF, HDEV, CAP = 128, 6, 2560, 1280, 192, 32
+MOVERS = 3
 GROUPS, GROUP_ROWS = 8, 24
 HID = 4 * HDEV
 SIZES = (CAP, CAP, CAP // 2, CAP // 2, CAP // 2, CAP // 2)
@@ -117,31 +118,85 @@
     )(d, w_in, w_out, g_in, g_out, got_in, got_out, f_in, s_in, f_out, s_out)
 
 
-def unpack_kernel(landed, f_in, s_in, f_out, s_out):
+def plan_kernel(place, plan, outgoing, crossing, incoming, flags, rank, mine):
+    def where_of(expert):
+        return expert % 16 // 2, expert // 16 * 2 + expert % 2
+
+    overflow = jnp.int32(0)
+    for z in range(NZ):
+        seen = jnp.int32(0)
+        for p in range(4):
+            rank[z * 4 + p] = seen
+            expert = p // 2 * 16 + z * 2 + p % 2
+            seen = seen + (plan[expert] != expert).astype(jnp.int32)
+        overflow = jnp.maximum(overflow, (seen > MOVERS).astype(jnp.int32))
+    for i in range(NZ * MOVERS):
+        crossing[i] = 0
+    for j in range(MOVERS):
+        mine[j] = 0
+    for z in range(NZ):
+        for p in range(4):
+            expert = p // 2 * 16 + z * 2 + p % 2
+            slot = rank[z * 4 + p]
+            counts = (plan[expert] != expert) & (slot < MOVERS)
+            from_z, from_p = where_of(plan[expert])
+            source = from_z * MOVERS + jnp.minimum(rank[from_z * 4 + from_p], MOVERS - 1)
+            crossing[jnp.where(counts, z * MOVERS + slot, NZ * MOVERS)] = source
+            mine[jnp.where(counts & (place[0] == z), slot, MOVERS)] = p
+    for z in range(NZ):
+        for j in range(MOVERS):
+            outgoing[z * MOVERS + j] = mine[j] * NZ + z
+        for p in range(4):
+            incoming[p * NZ + z] = z * MOVERS + jnp.minimum(rank[place[0] * 4 + p], MOVERS - 1)
+    expert = place[1]
+    flags[0] = (plan[expert] != expert).astype(jnp.int32)
+    flags[1] = overflow
+
+
+def plan_tables(place, plan):
+    scalar = pl.BlockSpec(memory_space=pltpu.SMEM)
+    return pl.pallas_call(
+        plan_kernel,
+        in_specs=[scalar] * 2,
+        out_specs=[scalar] * 4,
+        out_shape=[
+            jax.ShapeDtypeStruct((n,), jnp.int32) for n in (NZ * MOVERS, NZ * MOVERS + 1, NZ * 4, 2)
+        ],
+        scratch_shapes=[pltpu.SMEM((NZ * 4,), jnp.int32), pltpu.SMEM((MOVERS + 1,), jnp.int32)],
+        name="plan",
+    )(place, plan)
+
+
+def unpack_kernel(flags, landed, kept, f_in, s_in, f_out, s_out):
+    moves = flags[0] != 0
     for i, (inward, outward) in enumerate(((f_in, f_out), (s_in, s_out))):
         for m in range(3):
             for h in range(2):
-                part = landed[i, h, 0, m * GROUP_ROWS : (m + 1) * GROUP_ROWS]
+                rows = slice(m * GROUP_ROWS, (m + 1) * GROUP_ROWS)
+                part = jnp.where(moves, landed[i, h, 0, rows], kept[i, h, 0, rows])
                 if m < 2:
                     inward[m, :, h * 640 : (h + 1) * 640] = part
                 else:
                     outward[:, h * 640 : (h + 1) * 640] = part
 
 
-def unpack(landed):
+def unpack(flags, landed, kept):
     block = GROUP_ROWS
-    three = pl.BlockSpec((2, block, HALF), lambda i: (0, i, 0))
-    two = pl.BlockSpec((block, HALF), lambda i: (i, 0))
+    three = pl.BlockSpec((2, block, HALF), lambda i, f: (0, i, 0))
+    two = pl.BlockSpec((block, HALF), lambda i, f: (i, 0))
     inward = jax.ShapeDtypeStruct((2, HDEV, HALF), BF16)
     outward = jax.ShapeDtypeStruct((HDEV, HALF), BF16)
     return pl.pallas_call(
         unpack_kernel,
-        grid=(GROUPS,),
-        in_specs=[pl.BlockSpec((2, 2, 1, 3 * block, 640), lambda i: (0, 0, i, 0, 0))],
-        out_specs=[three, three, two, two],
+        grid_spec=pltpu.PrefetchScalarGridSpec(
+            num_scalar_prefetch=1,
+            grid=(GROUPS,),
+            in_specs=[pl.BlockSpec((2, 2, 1, 3 * block, 640), lambda i, f: (0, 0, i, 0, 0))] * 2,
+            out_specs=[three, three, two, two],
+        ),
         out_shape=[inward, inward, outward, outward],
         name="unpack",
-    )(landed)
+    )(flags, landed, kept)
 
 
 def select_kernel(count, experts, *refs):
@@ -358,14 +413,24 @@
     far_got = spread_out(far_rows)
 
     plane, piece = ("yl", "xp"), (3 * GROUP_ROWS, 640)
+
+    def rows_at(array, index, *shape):
+        return array.reshape(-1, *piece).at[index].get(mode="promise_in_bounds").reshape(*shape, *piece)
+
+    place = jnp.stack([z, yl * 16 + z * 2 + xp]).astype(jnp.int32)
+    outgoing, crossing, incoming, flags = plan_tables(place, owner_plan)
     spread = exchange(moments.reshape(4, GROUPS, *piece), plane)
-    spread = exchange(spread.transpose(1, 0, 2, 3), "z").reshape(NZ * 4, *piece)
-    source = owner_plan.reshape(2, NZ, 2).transpose(1, 0, 2).reshape(NZ * 4)
-    source = source % 16 // 2 * 4 + source // 16 * 2 + source % 2
-    picked = spread.at[source].get(mode="promise_in_bounds").reshape(NZ, 4, *piece)
-    landed = exchange(picked, "z").transpose(1, 0, 2, 3)
-    landed = exchange(landed, plane)
-    next_moments = unpack(landed.reshape(2, 2, GROUPS, *piece))
+    spread = exchange(rows_at(spread, outgoing, NZ, MOVERS), "z")
+    landed = exchange(rows_at(spread, crossing[: NZ * MOVERS], NZ, MOVERS), "z")
+    landed = exchange(rows_at(landed, incoming, 4, NZ), plane)
+
+    def all_move(landed, moments):
+        everywhere = ("yl", "z", "xp")
+        spread = exchange(moments.reshape(32, *piece), everywhere)
+        return exchange(rows_at(spread, owner_plan, 32), everywhere).reshape(landed.shape)
+
+    landed = lax.cond(flags[1] != 0, all_move, lambda landed, moments: landed, landed, moments)
+    next_moments = unpack(flags, landed.reshape(2, 2, GROUPS, *piece), moments)
 
     far_done = ffn(pieces, far_got)
     far_back = spread_out(far_done)

time: 527 us -> 516 us (0.979)
  waiting for transfers between devices: 320 us -> 285 us
  starting transfers between devices: 96.9 us -> 113 us
    ppermute x16, waiting for transfers between devices: 159 us -> 120 us  [along_z(): return lax.ppermute(a, 'z', [(i, (i + step) % NZ) for i in range(NZ)])]
    ppermute x17, waiting for transfers between devices: 58.3 us -> 86.8 us  [permute(): return lax.ppermute(a, axis, SWAP)]
    all_to_all x4, waiting for transfers between devices: 51.4 us -> 25.4 us  [exchange(): return lax.all_to_all(a, axes, 0, 0, tiled=True)]
    ppermute x16, starting transfers between devices: 26.2 us -> 36.3 us  [along_z(): return lax.ppermute(a, 'z', [(i, (i + step) % NZ) for i in range(NZ)])]
    ppermute x4, starting transfers between devices: 4.8 us -> 12.4 us  [to_outer_diagonal(): return lax.ppermute(a, ('yl', 'xp', 'xq', 'dp'), OUTER_DIAGONAL)]
    ppermute x4, waiting for transfers between devices: 14.9 us -> 20.6 us  [to_outer_diagonal(): return lax.ppermute(a, ('yl', 'xp', 'xq', 'dp'), OUTER_DIAGONAL)]
  transfers between devices with their start and end apart: 57 -> 57, of which waited for: 24 -> 24; matrix products, arithmetic and copies ran while one was open for 6% -> 6% of each run, Pallas kernels for 9% -> 12%
where the time goes in v1:
time: 516 us; the launch traced here: 507 us
  waiting for transfers between devices  285 us (55%)
  starting transfers between devices  113 us (22%)
  Pallas kernels  65.7 us (13%)
  local copies, waits for them, and re-layouts  23.7 us (5%)
  other arithmetic  17.9 us (3%)
    ppermute x16, waiting for transfers between devices, along_z(): return lax.ppermute(a, 'z', [(i, (i + step) % NZ) for i in range(NZ)])  120 us
    ppermute x17, waiting for transfers between devices, permute(): return lax.ppermute(a, axis, SWAP)  86.8 us
    ppermute x16, starting transfers between devices, along_z(): return lax.ppermute(a, 'z', [(i, (i + step) % NZ) for i in range(NZ)])  36.3 us
    ppermute x4, waiting for transfers between devices, to_diagonal(): return lax.ppermute(a, ('yl', 'xp', 'xq'), DIAGONAL)  30.3 us
    pallas_call x2, Pallas kernels, ffn(): pl.pallas_call(lambda *refs: ffn_kernel(count, *refs), in_specs=[anywhere...  28.9 us
    all_to_all x4, waiting for transfers between devices, exchange(): return lax.all_to_all(a, axes, 0, 0, tiled=True)  25.4 us
    all_to_all x4, starting transfers between devices, exchange(): return lax.all_to_all(a, axes, 0, 0, tiled=True)  24.4 us
    ppermute x4, waiting for transfers between devices, to_outer_diagonal(): return lax.ppermute(a, ('yl', 'xp', 'xq', 'dp'), OUTER_DIAGONAL)  20.6 us
  transfers between devices with their start and end apart: 57, of which 24 were waited for; matrix products, arithmetic and copies ran while one was open for 6% of the time, Pallas kernels for 12%

profile of v1, /device:TPU:8, one launch (start us, length us, event | category | flops | bytes accessed | tf_op | source)
XLA Modules:
  0.0 506.9 jit_solution(11875357297689746475)
XLA Ops:
  14.4 24.7 %collective-permute-done.5.got_out = bf16[192,1280]{1,0:T(8,128)(2,1)S(1)} collective-permute-done((bf16[192,1280]{1,0:T(8,128)(2,1)S(1)}, bf16[192,1280]{1,0:T(8,128)(2,1)S(1)}, u32[]{:S(2)}, u32[]{:S(2)}) %collective-permute-start.5) | collective-permute-done | bytes 491552 | tf_op jit(solution)/shard_map/ppermute | solution.py:372
  40.1 9.3 %adam.1 = (bf16[3,192,1280]{2,1,0:T(8,128)(2,1)}, bf16[2,2,8,72,640]{4,3,2,1,0:T(8,128)(2,1)}, bf16[192,1280]{1,0:T(8,128)(2,1)}, bf16[192,1280]{1,0:T(8,128)(2,1)}, bf16[192,1280]{1,0:T(8,128)(2,1)}) custom-call(s32[1]{0:T(128)} %bitcast.7.d_ref, bf16[2,192,1280]{2,1,0:T(8,128)(2,1)} %w_in.1, bf16[192,1280]{1,0:T(8,128)(2,1)} %w_out.1, ...), custom_call_target="tpu_custom_call" | custom-call | tf_op jit(solution)/shard_map/adam/pallas_call | solution.py:87
  49.4 5.8 %all-to-all-start.2 = ((bf16[4,8,72,640]{3,2,1,0:T(8,128)(2,1)}), bf16[4,8,72,640]{3,2,1,0:T(8,128)(2,1)S(1)}, u32[]{:S(2)}, u32[]{:S(2)}) async-start(bf16[4,8,72,640]{3,2,1,0:T(8,128)(2,1)} %bitcast.12), calls=%async_computation.2 | async-start | bytes 5898240 | tf_op jit(solution)/shard_map/all_to_all | solution.py:55
  65.2 10.2 %collective-permute-done.2.refs_4_ = bf16[128,2688]{1,0:T(8,128)(2,1)} collective-permute-done((bf16[128,2688]{1,0:T(8,128)(2,1)}, bf16[128,2688]{1,0:T(8,128)(2,1)}, u32[]{:S(2)}, u32[]{:S(2)}) %collective-permute-start.2) | collective-permute-done | bytes 688160 | tf_op jit(solution)/shard_map/ppermute | solution.py:59
  77.7 23.7 %collective-permute-done.9.refs_4_ = bf16[192,1280]{1,0:T(8,128)(2,1)S(1)} collective-permute-done((bf16[192,1280]{1,0:T(8,128)(2,1)}, bf16[192,1280]{1,0:T(8,128)(2,1)S(1)}, u32[]{:S(2)}, u32[]{:S(2)}) %collective-permute-start.9) | collective-permute-done | bytes 491552 | tf_op jit(solution)/shard_map/ppermute | solution.py:372
  102.0 9.9 %collective-permute-done.10.refs_5_ = bf16[192,1280]{1,0:T(8,128)(2,1)S(1)} collective-permute-done((bf16[192,1280]{1,0:T(8,128)(2,1)}, bf16[192,1280]{1,0:T(8,128)(2,1)S(1)}, u32[]{:S(2)}, u32[]{:S(2)}) %collective-permute-start.10) | collective-permute-done | bytes 491552 | tf_op jit(solution)/shard_map/ppermute | solution.py:372
  114.4 5.9 %collective-permute-done.11.refs_6_ = bf16[192,1280]{1,0:T(8,128)(2,1)} collective-permute-done((bf16[192,1280]{1,0:T(8,128)(2,1)}, bf16[192,1280]{1,0:T(8,128)(2,1)}, u32[]{:S(2)}, u32[]{:S(2)}) %collective-permute-start.11) | collective-permute-done | bytes 491552 | tf_op jit(solution)/shard_map/ppermute | solution.py:372
  120.9 10.4 %collective-permute-done.12.refs_7_ = bf16[192,1280]{1,0:T(8,128)(2,1)S(1)} collective-permute-done((bf16[192,1280]{1,0:T(8,128)(2,1)S(1)}, bf16[192,1280]{1,0:T(8,128)(2,1)S(1)}, u32[]{:S(2)}, u32[]{:S(2)}) %collective-permute-start.12) | collective-permute-done | bytes 491552 | tf_op jit(solution)/shard_map/ppermute | solution.py:372
  131.3 10.5 %collective-permute-done.13.refs_8_ = bf16[192,1280]{1,0:T(8,128)(2,1)S(1)} collective-permute-done((bf16[192,1280]{1,0:T(8,128)(2,1)S(1)}, bf16[192,1280]{1,0:T(8,128)(2,1)S(1)}, u32[]{:S(2)}, u32[]{:S(2)}) %collective-permute-start.13) | collective-permute-done | bytes 491552 | tf_op jit(solution)/shard_map/ppermute | solution.py:372
  142.6 5.9 %collective-permute-start.32 = (bf16[128,2688]{1,0:T(8,128)(2,1)}, bf16[128,2688]{1,0:T(8,128)(2,1)}, u32[]{:S(2)}, u32[]{:S(2)}) collective-permute-start(bf16[128,2688]{1,0:T(8,128)(2,1)} %collective-permute-done.3.refs_5_), channel_id=1, source_target_pairs={{0,112},{16,0},{32,16},{48,32},{64,48},{80,64},{96,80},{112,96},{1... | collective-permute-start | bytes 2064392 | tf_op jit(solution)/shard_map/ppermute | solution.py:59
  161.7 6.8 %all-to-all-start.3 = ((bf16[8,3,72,640]{3,2,1,0:T(8,128)(2,1)}), bf16[8,3,72,640]{3,2,1,0:T(8,128)(2,1)S(1)}, u32[]{:S(2)}, u32[]{:S(2)}) async-start(bf16[8,3,72,640]{3,2,1,0:T(8,128)(2,1)} %bitcast.25), calls=%async_computation.3 | async-start | bytes 4423680 | tf_op jit(solution)/shard_map/all_to_all | solution.py:55
  174.6 51.0 %collective-permute-done.34 = bf16[64,2688]{1,0:T(8,128)(2,1)S(1)} collective-permute-done((bf16[64,2688]{1,0:T(8,128)(2,1)}, bf16[64,2688]{1,0:T(8,128)(2,1)S(1)}, u32[]{:S(2)}, u32[]{:S(2)}) %collective-permute-start.34) | collective-permute-done | bytes 344096 | tf_op jit(solution)/shard_map/ppermute | solution.py:59
  244.5 9.7 %collective-permute-done.38.refs_20_ = bf16[48,2560]{1,0:T(8,128)(2,1)S(1)} collective-permute-done((bf16[48,2560]{1,0:T(8,128)(2,1)}, bf16[48,2560]{1,0:T(8,128)(2,1)S(1)}, u32[]{:S(2)}, u32[]{:S(2)}) %collective-permute-start.38) | collective-permute-done | bytes 245792 | tf_op jit(solution)/shard_map/ppermute | solution.py:43
  261.0 13.5 %shard_map.159 = (bf16[96,2560]{1,0:T(8,128)(2,1)}, bf16[96,2560]{1,0:T(8,128)(2,1)}, bf16[48,2560]{1,0:T(8,128)(2,1)}, bf16[48,2560]{1,0:T(8,128)(2,1)}, bf16[4...) custom-call(bf16[3,192,1280]{2,1,0:T(8,128)(2,1)} %get-tuple-element.68.refs_0_, ...), custom_call_target="tpu_custom_call" | custom-call | tf_op jit(solution)/shard_map/pallas_call | solution.py:333
  284.3 6.1 %shard_map.155 = (bf16[160,2560]{1,0:T(8,128)(2,1)}, bf16[160,2560]{1,0:T(8,128)(2,1)}, bf16[80,2560]{1,0:T(8,128)(2,1)}, bf16[80,2560]{1,0:T(8,128)(2,1)}, bf16...) custom-call(s32[4]{0:T(128)} %pad_add_fusion.refs_0_, ...), custom_call_target="tpu_custom_call" | custom-call | tf_op jit(solution)/shard_map/pallas_call | solution.py:239
  313.6 14.2 %collective-permute-done.24.refs_20_ = bf16[80,2560]{1,0:T(8,128)(2,1)} collective-permute-done((bf16[80,2560]{1,0:T(8,128)(2,1)}, bf16[80,2560]{1,0:T(8,128)(2,1)}, u32[]{:S(2)}, u32[]{:S(2)}) %collective-permute-start.24) | collective-permute-done | bytes 409632 | tf_op jit(solution)/shard_map/ppermute | solution.py:43
  327.8 6.0 %collective-permute-done.25.refs_21_ = bf16[80,2560]{1,0:T(8,128)(2,1)} collective-permute-done((bf16[80,2560]{1,0:T(8,128)(2,1)}, bf16[80,2560]{1,0:T(8,128)(2,1)}, u32[]{:S(2)}, u32[]{:S(2)}) %collective-permute-start.25) | collective-permute-done | bytes 409632 | tf_op jit(solution)/shard_map/ppermute | solution.py:51
  334.6 15.4 %shard_map.156 = (bf16[160,2560]{1,0:T(8,128)(2,1)}, bf16[160,2560]{1,0:T(8,128)(2,1)}, bf16[80,2560]{1,0:T(8,128)(2,1)}, bf16[80,2560]{1,0:T(8,128)(2,1)}, bf16...) custom-call(bf16[3,192,1280]{2,1,0:T(8,128)(2,1)} %get-tuple-element.68.refs_0_, ...), custom_call_target="tpu_custom_call" | custom-call | tf_op jit(solution)/shard_map/pallas_call | solution.py:333
  365.5 6.9 %all-to-all-start.4 = ((bf16[8,3,72,640]{3,2,1,0:T(8,128)(2,1)}), bf16[8,3,72,640]{3,2,1,0:T(8,128)(2,1)S(1)}, u32[]{:S(2)}, u32[]{:S(2)}) async-start(bf16[8,3,72,640]{3,2,1,0:T(8,128)(2,1)} %bitcast.26), calls=%async_computation.4 | async-start | bytes 4423680 | tf_op jit(solution)/shard_map/all_to_all | solution.py:55
  383.4 5.9 %collective-permute-done.30.refs_7_ = bf16[80,2560]{1,0:T(8,128)(2,1)S(1)} collective-permute-done((bf16[80,2560]{1,0:T(8,128)(2,1)}, bf16[80,2560]{1,0:T(8,128)(2,1)S(1)}, u32[]{:S(2)}, u32[]{:S(2)}) %collective-permute-start.30) | collective-permute-done | bytes 409632 | tf_op jit(solution)/shard_map/ppermute | solution.py:51
  395.7 39.7 %collective-permute-done.46 = bf16[128,2560]{1,0:T(8,128)(2,1)} collective-permute-done((bf16[128,2560]{1,0:T(8,128)(2,1)}, bf16[128,2560]{1,0:T(8,128)(2,1)}, u32[]{:S(2)}, u32[]{:S(2)}) %collective-permute-start.46) | collective-permute-done | bytes 655392 | tf_op jit(solution)/shard_map/ppermute | solution.py:59
  441.6 12.2 %collective-permute-done.47 = bf16[128,2560]{1,0:T(8,128)(2,1)S(1)} collective-permute-done((bf16[128,2560]{1,0:T(8,128)(2,1)S(1)}, bf16[128,2560]{1,0:T(8,128)(2,1)S(1)}, u32[]{:S(2)}, u32[]{:S(2)}) %collective-permute-start.47) | collective-permute-done | bytes 655392 | tf_op jit(solution)/shard_map/ppermute | solution.py:59
  474.5 25.4 %all-to-all-done.5 = bf16[4,8,72,640]{3,2,1,0:T(8,128)(2,1)S(1)} async-done(((bf16[4,8,72,640]{3,2,1,0:T(8,128)(2,1)}), bf16[4,8,72,640]{3,2,1,0:T(8,128)(2,1)S(1)}, u32[]{:S(2)}, u32[]{:S(2)}) %all-to-all-start.5) | async-done | bytes 2949152 | tf_op jit(solution)/shard_map/all_to_all | solution.py:55
  499.9 6.8 %unpack.1 = (bf16[2,192,1280]{2,1,0:T(8,128)(2,1)}, bf16[2,192,1280]{2,1,0:T(8,128)(2,1)}, bf16[192,1280]{1,0:T(8,128)(2,1)}, bf16[192,1280]{1,0:T(8,128)(2,1)}) custom-call(s32[2]{0:T(128)} %get-tuple-element.106.flags, bf16[2,2,8,72,640]{4,3,2,1,0:T(8,128)(2,1)S(1)} %get-tuple-element.123.landed, bf16[2,2,8,72,640]{4,3,2,1,0:T(8,128)(2,1)} %get-tuple-element.107.kept), custom_call_target="tpu_custom_call" | custom-call | tf_op jit(solution)/shard_map/unpack/pallas_call | solution.py:189
  (200 shorter events, 169.3 us)
Async XLA Ops:
  3.3 35.7 %collective-permute-start.4 = (bf16[2,192,1280]{2,1,0:T(8,128)(2,1)}, bf16[2,192,1280]{2,1,0:T(8,128)(2,1)S(1)}, u32[]{:S(2)}, u32[]{:S(2)}) collective-permute-start(bf16[2,192,1280]{2,1,0:T(8,128)(2,1)} %slice_select_fusion), channel_id=1, source_target_pairs={{0,1},{1,0},{2,3},{3,2},{4,5},{5,4},{6,7},{7,6},{8,9},{9,8},{10,11... | collective-permute-start | bytes 2949128 | tf_op jit(solution)/shard_map/ppermute | solution.py:372
  7.1 48.1 %collective-permute-start = (bf16[128,2688]{1,0:T(8,128)(2,1)}, bf16[128,2688]{1,0:T(8,128)(2,1)}, u32[]{:S(2)}, u32[]{:S(2)}) collective-permute-start(bf16[128,2688]{1,0:T(8,128)(2,1)} %concatenate.15.refs_1_), channel_id=1, source_target_pairs={{0,16},{16,32},{32,48},{48,64},{64,80},{80,96},{96,112},{112,0},{1... | collective-permute-start | bytes 2064392 | tf_op jit(solution)/shard_map/ppermute | solution.py:59
  10.4 50.8 %collective-permute-start.1 = (bf16[128,2688]{1,0:T(8,128)(2,1)}, bf16[128,2688]{1,0:T(8,128)(2,1)}, u32[]{:S(2)}, u32[]{:S(2)}) collective-permute-start(bf16[128,2688]{1,0:T(8,128)(2,1)} %concatenate.15.refs_1_), channel_id=1, source_target_pairs={{0,112},{16,0},{32,16},{48,32},{64,48},{80,64},{96,80},{112,96},{1... | collective-permute-start | bytes 2064392 | tf_op jit(solution)/shard_map/ppermute | solution.py:59
  49.4 109.8 %all-to-all-start.2 = ((bf16[4,8,72,640]{3,2,1,0:T(8,128)(2,1)}), bf16[4,8,72,640]{3,2,1,0:T(8,128)(2,1)S(1)}, u32[]{:S(2)}, u32[]{:S(2)}) async-start(bf16[4,8,72,640]{3,2,1,0:T(8,128)(2,1)} %bitcast.12), calls=%async_computation.2 | async-start | bytes 5898240 | tf_op jit(solution)/shard_map/all_to_all | solution.py:55
  57.1 44.2 %collective-permute-start.9 = (bf16[192,1280]{1,0:T(8,128)(2,1)}, bf16[192,1280]{1,0:T(8,128)(2,1)S(1)}, u32[]{:S(2)}, u32[]{:S(2)}) collective-permute-start(bf16[192,1280]{1,0:T(8,128)(2,1)} %get-tuple-element.69), channel_id=1, source_target_pairs={{0,1},{1,0},{2,3},{3,2},{4,5},{5,4},{6,7},{7,6},{8,9},{9,8},{10,11... | collective-permute-start | bytes 1474568 | tf_op jit(solution)/shard_map/ppermute | solution.py:372
  59.4 94.1 %collective-permute-start.6 = (bf16[3,192,1280]{2,1,0:T(8,128)(2,1)}, bf16[3,192,1280]{2,1,0:T(8,128)(2,1)}, u32[]{:S(2)}, u32[]{:S(2)}) collective-permute-start(bf16[3,192,1280]{2,1,0:T(8,128)(2,1)} %get-tuple-element.68.refs_0_), channel_id=1, source_target_pairs={{0,4},{4,0},{1,5},{5,1},{2,6},{6,2},{3,7},{7,3},{8,12},{12,8},{9,1... | collective-permute-start | bytes 4423688 | tf_op jit(solution)/shard_map/ppermute | solution.py:372
  60.0 51.9 %collective-permute-start.10 = (bf16[192,1280]{1,0:T(8,128)(2,1)}, bf16[192,1280]{1,0:T(8,128)(2,1)S(1)}, u32[]{:S(2)}, u32[]{:S(2)}) collective-permute-start(bf16[192,1280]{1,0:T(8,128)(2,1)} %get-tuple-element.70), channel_id=1, source_target_pairs={{0,1},{1,0},{2,3},{3,2},{4,5},{5,4},{6,7},{7,6},{8,9},{9,8},{10,11... | collective-permute-start | bytes 1474568 | tf_op jit(solution)/shard_map/ppermute | solution.py:372
  61.2 51.3 %collective-permute-start.3 = (bf16[128,2688]{1,0:T(8,128)(2,1)}, bf16[128,2688]{1,0:T(8,128)(2,1)}, u32[]{:S(2)}, u32[]{:S(2)}) collective-permute-start(bf16[128,2688]{1,0:T(8,128)(2,1)} %collective-permute-done.1.refs_3_), channel_id=1, source_target_pairs={{0,112},{16,0},{32,16},{48,32},{64,48},{80,64},{96,80},{112,96},{1... | collective-permute-start | bytes 2064392 | tf_op jit(solution)/shard_map/ppermute | solution.py:59
  75.4 44.9 %collective-permute-start.11 = (bf16[192,1280]{1,0:T(8,128)(2,1)}, bf16[192,1280]{1,0:T(8,128)(2,1)}, u32[]{:S(2)}, u32[]{:S(2)}) collective-permute-start(bf16[192,1280]{1,0:T(8,128)(2,1)} %get-tuple-element.71), channel_id=1, source_target_pairs={{0,1},{1,0},{2,3},{3,2},{4,5},{5,4},{6,7},{7,6},{8,9},{9,8},{10,11... | collective-permute-start | bytes 1474568 | tf_op jit(solution)/shard_map/ppermute | solution.py:372
  112.5 40.9 %collective-permute-start.31 = (bf16[128,2688]{1,0:T(8,128)(2,1)}, bf16[128,2688]{1,0:T(8,128)(2,1)}, u32[]{:S(2)}, u32[]{:S(2)}) collective-permute-start(bf16[128,2688]{1,0:T(8,128)(2,1)} %collective-permute-done.2.refs_4_), channel_id=1, source_target_pairs={{0,16},{16,32},{32,48},{48,64},{64,80},{80,96},{96,112},{112,0},{1... | collective-permute-start | bytes 2064392 | tf_op jit(solution)/shard_map/ppermute | solution.py:59
  150.2 87.6 %collective-permute-start.7 = (bf16[3,192,1280]{2,1,0:T(8,128)(2,1)}, bf16[3,192,1280]{2,1,0:T(8,128)(2,1)}, u32[]{:S(2)}, u32[]{:S(2)}) collective-permute-start(bf16[3,192,1280]{2,1,0:T(8,128)(2,1)} %get-tuple-element.68.refs_0_), channel_id=1, source_target_pairs={{0,2},{2,0},{1,3},{3,1},{4,6},{6,4},{5,7},{7,5},{8,10},{10,8},{9,1... | collective-permute-start | bytes 4423688 | tf_op jit(solution)/shard_map/ppermute | solution.py:372
  153.5 106.8 %collective-permute-start.8 = (bf16[3,192,1280]{2,1,0:T(8,128)(2,1)}, bf16[3,192,1280]{2,1,0:T(8,128)(2,1)}, u32[]{:S(2)}, u32[]{:S(2)}) collective-permute-start(bf16[3,192,1280]{2,1,0:T(8,128)(2,1)} %collective-permute-done.6.refs_1_), channel_id=1, source_target_pairs={{0,2},{2,0},{1,3},{3,1},{4,6},{6,4},{5,7},{7,5},{8,10},{10,8},{9,1... | collective-permute-start | bytes 4423688 | tf_op jit(solution)/shard_map/ppermute | solution.py:372
  161.7 201.4 %all-to-all-start.3 = ((bf16[8,3,72,640]{3,2,1,0:T(8,128)(2,1)}), bf16[8,3,72,640]{3,2,1,0:T(8,128)(2,1)S(1)}, u32[]{:S(2)}, u32[]{:S(2)}) async-start(bf16[8,3,72,640]{3,2,1,0:T(8,128)(2,1)} %bitcast.25), calls=%async_computation.3 | async-start | bytes 4423680 | tf_op jit(solution)/shard_map/all_to_all | solution.py:55
  170.2 55.4 %collective-permute-start.34 = (bf16[64,2688]{1,0:T(8,128)(2,1)}, bf16[64,2688]{1,0:T(8,128)(2,1)S(1)}, u32[]{:S(2)}, u32[]{:S(2)}) collective-permute-start(bf16[64,2688]{1,0:T(8,128)(2,1)} %slice.57), channel_id=1, source_target_pairs={{0,112},{16,0},{32,16},{48,32},{64,48},{80,64},{96,80},{112,96},{1... | collective-permute-start | bytes 1032200 | tf_op jit(solution)/shard_map/ppermute | solution.py:59
  173.5 58.4 %collective-permute-start.18 = (bf16[192,1280]{1,0:T(8,128)(2,1)S(1)}, bf16[192,1280]{1,0:T(8,128)(2,1)}, u32[]{:S(2)}, u32[]{:S(2)}) collective-permute-start(bf16[192,1280]{1,0:T(8,128)(2,1)S(1)} %copy-done.4), channel_id=1, source_target_pairs={{0,2},{2,0},{1,3},{3,1},{4,6},{6,4},{5,7},{7,5},{8,10},{10,8},{9,1... | collective-permute-start | bytes 1474568 | tf_op jit(solution)/shard_map/ppermute | solution.py:372
  173.5 58.7 %collective-permute-start.19 = (bf16[192,1280]{1,0:T(8,128)(2,1)S(1)}, bf16[192,1280]{1,0:T(8,128)(2,1)}, u32[]{:S(2)}, u32[]{:S(2)}) collective-permute-start(bf16[192,1280]{1,0:T(8,128)(2,1)S(1)} %copy-done.6), channel_id=1, source_target_pairs={{0,2},{2,0},{1,3},{3,1},{4,6},{6,4},{5,7},{7,5},{8,10},{10,8},{9,1... | collective-permute-start | bytes 1474568 | tf_op jit(solution)/shard_map/ppermute | solution.py:372
  274.6 30.5 %collective-permute-start.40 = (bf16[96,2560]{1,0:T(8,128)(2,1)}, bf16[96,2560]{1,0:T(8,128)(2,1)S(1)}, u32[]{:S(2)}, u32[]{:S(2)}) collective-permute-start(bf16[96,2560]{1,0:T(8,128)(2,1)} %get-tuple-element.96), channel_id=1, source_target_pairs={{0,12},{12,0},{4,8},{8,4},{1,13},{13,1},{5,9},{9,5},{2,14},{14,2},... | collective-permute-start | bytes 1474568 | tf_op jit(solution)/shard_map/ppermute | solution.py:35
  291.2 42.6 %collective-permute-start.21 = (bf16[160,2560]{1,0:T(8,128)(2,1)}, bf16[160,2560]{1,0:T(8,128)(2,1)S(1)}, u32[]{:S(2)}, u32[]{:S(2)}) collective-permute-start(bf16[160,2560]{1,0:T(8,128)(2,1)} %get-tuple-element.73), channel_id=1, source_target_pairs={{0,12},{12,0},{4,8},{8,4},{1,13},{13,1},{5,9},{9,5},{2,14},{14,2},... | collective-permute-start | bytes 2457608 | tf_op jit(solution)/shard_map/ppermute | solution.py:35
  311.7 47.8 %collective-permute-start.45 = (bf16[64,2560]{1,0:T(8,128)(2,1)}, bf16[64,2560]{1,0:T(8,128)(2,1)}, u32[]{:S(2)}, u32[]{:S(2)}) collective-permute-start(bf16[64,2560]{1,0:T(8,128)(2,1)} %get-tuple-element.119), channel_id=1, source_target_pairs={{0,16},{16,32},{32,48},{48,64},{64,80},{80,96},{96,112},{112,0},{1... | collective-permute-start | bytes 983048 | tf_op jit(solution)/shard_map/ppermute | solution.py:59
  350.0 39.3 %collective-permute-start.26 = (bf16[160,2560]{1,0:T(8,128)(2,1)}, bf16[160,2560]{1,0:T(8,128)(2,1)S(1)}, u32[]{:S(2)}, u32[]{:S(2)}) collective-permute-start(bf16[160,2560]{1,0:T(8,128)(2,1)} %get-tuple-element.79), channel_id=1, source_target_pairs={{0,12},{12,0},{4,8},{8,4},{1,13},{13,1},{5,9},{9,5},{2,14},{14,2},... | collective-permute-start | bytes 2457608 | tf_op jit(solution)/shard_map/ppermute | solution.py:35
  365.5 93.8 %all-to-all-start.4 = ((bf16[8,3,72,640]{3,2,1,0:T(8,128)(2,1)}), bf16[8,3,72,640]{3,2,1,0:T(8,128)(2,1)S(1)}, u32[]{:S(2)}, u32[]{:S(2)}) async-start(bf16[8,3,72,640]{3,2,1,0:T(8,128)(2,1)} %bitcast.26), calls=%async_computation.4 | async-start | bytes 4423680 | tf_op jit(solution)/shard_map/all_to_all | solution.py:55
  375.2 60.1 %collective-permute-start.46 = (bf16[128,2560]{1,0:T(8,128)(2,1)}, bf16[128,2560]{1,0:T(8,128)(2,1)}, u32[]{:S(2)}, u32[]{:S(2)}) collective-permute-start(bf16[128,2560]{1,0:T(8,128)(2,1)} %pad_maximum_fusion.1), channel_id=1, source_target_pairs={{0,16},{16,32},{32,48},{48,64},{64,80},{80,96},{96,112},{112,0},{1... | collective-permute-start | bytes 1966088 | tf_op jit(solution)/shard_map/ppermute | solution.py:59
  379.2 57.7 %collective-permute-start.50 = (bf16[128,2560]{1,0:T(8,128)(2,1)}, bf16[128,2560]{1,0:T(8,128)(2,1)}, u32[]{:S(2)}, u32[]{:S(2)}) collective-permute-start(bf16[128,2560]{1,0:T(8,128)(2,1)} %pad_maximum_fusion.2), channel_id=1, source_target_pairs={{0,112},{16,0},{32,16},{48,32},{64,48},{80,64},{96,80},{112,96},{1... | collective-permute-start | bytes 1966088 | tf_op jit(solution)/shard_map/ppermute | solution.py:59
  462.0 38.0 %all-to-all-start.5 = ((bf16[4,8,72,640]{3,2,1,0:T(8,128)(2,1)}), bf16[4,8,72,640]{3,2,1,0:T(8,128)(2,1)S(1)}, u32[]{:S(2)}, u32[]{:S(2)}) async-start(bf16[4,8,72,640]{3,2,1,0:T(8,128)(2,1)} %bitcast.22), calls=%async_computation.5 | async-start | bytes 5898240 | tf_op jit(solution)/shard_map/all_to_all | solution.py:55
  (63 other events, 1034.6 us)
